TPU v7x, 32 devices: a whole 2x2x4 slice. The times are simulated.
32 devices in a mesh: dom: 8 (over z, x), feat: 4 (over y, core).
Axes of the slice: x: 2, y: 2, z: 4, core: 2. Of those that a mesh axis runs over, the one named last changes fastest.
Arguments:
- feats: bfloat16 [256, 4096], P('feat', 'dom'), may hold values from -6 to 6
- self_weight: bfloat16 [256, 256], P(None, 'feat'), may hold values from -0.375 to 0.375
- bases: bfloat16 [30, 256, 256], P(None, 'feat'), may hold values from -0.375 to 0.375
- coef: float32 [237, 30], replicated, may hold values from -1.2 to 1.2
- src_part: int32 [8192, 1], P('dom'), may hold values from 0 to 7; in each aligned block of 1024 rows (0 to 1023, 1024 to 2047, ...) at most 256 rows name the same one
- src_row: int32 [8192], P('dom'), may hold values from 0 to 511
- edge_dst: int32 [8192], P('dom'), may hold values from 0 to 511
- edge_rel: int32 [8192], P('dom'), may hold values from 0 to 236
- block_owner: int32 [64, 1], P('dom'), may hold values from 0 to 7; in each aligned block of 8 rows (0 to 7, 8 to 15, ...) at most 2 rows name the same one
- block_valid: int32 [8, 8], P('dom'), may hold values from 1 to 128, 896 in all within a row
- cotangent: bfloat16 [256, 4096], P('feat', 'dom'), may hold values from -6 to 6
Outputs:
- output: bfloat16 [256, 4096], P('feat', 'dom')
- grad_feats: bfloat16 [256, 4096], P('feat', 'dom')
- grad_bases: float32 [30, 256, 256], P(None, 'feat')
- grad_self: float32 [256, 256], P(None, 'feat')
- grad_coef: float32 [237, 30], replicated
Inputs may be any that keep to these rules, and one draw needn't show every extreme that they name: `src_part`: among the edge rows of one index of dom, no partition is the source partition of more than 256 rows, and some partition of exactly 256. `block_owner`: among the blocks of one index of dom, no partition owns more than 2, a bound that some block reaches. `block_valid`: the valid rows of a block come first; the counts of one index of dom sum to 896.
All inputs are finite; a program needn't handle non-finite values.
Results may differ from a plain program's by a relative error of at most 0.0055.
Values may be sent and summed in bfloat16 or wider, within the bound.
A program may use at most 64 MiB of HBM per device.

v0:
```python
import jax
import jax.numpy as jnp
from jax import lax
from jax.sharding import PartitionSpec as P

BF = jnp.bfloat16
F32 = jnp.float32


def dot(left, right, left_axis, right_axis):
    return lax.dot_general(
        left, right, (((left_axis,), (right_axis,)), ((), ())), preferred_element_type=F32
    )


def onehot(ids, start, size):
    return (jnp.arange(size, dtype=jnp.int32)[:, None] + start == ids[None, :]).astype(BF)


def pick(table, ids, chunk):
    width = table.shape[1]
    if width <= chunk:
        return dot(table, onehot(ids, 0, width), 1, 0).astype(BF)

    def step(index, total):
        piece = lax.dynamic_slice_in_dim(table, index * chunk, chunk, 1)
        return total + dot(piece, onehot(ids, index * chunk, chunk), 1, 0)

    total = lax.fori_loop(0, width // chunk, step, jnp.zeros((table.shape[0], ids.shape[0]), F32))
    return total.astype(BF)


def spread(values, ids, width, chunk):
    if width <= chunk:
        return dot(values, onehot(ids, 0, width), 1, 1)

    def step(index, total):
        piece = dot(values, onehot(ids, index * chunk, chunk), 1, 1)
        return lax.dynamic_update_slice_in_dim(total, piece, index * chunk, 1)

    return lax.fori_loop(0, width // chunk, step, jnp.zeros((values.shape[0], width), F32))


def scatter_sum(values, axis, count):
    rows = values.shape[0]
    parts = lax.all_to_all(values, axis, split_axis=1, concat_axis=0, tiled=True)
    return jnp.sum(parts.reshape(count, rows, -1).astype(F32), axis=0)


def body(
    feats,
    self_weight,
    bases,
    coef,
    src_part,
    src_row,
    edge_dst,
    edge_rel,
    block_owner,
    block_valid,
    cotangent,
):
    dom_count = lax.axis_size("dom")
    feat_count = lax.axis_size("feat")
    quarter, entities = feats.shape
    edge_count = src_row.shape[0]
    block_count = block_valid.shape[1]
    block_rows = edge_count // block_count
    basis_count, _, width = bases.shape
    relations = coef.shape[0]
    total_entities = dom_count * entities
    chunk = min(8, dom_count) * entities
    scale = float(edge_count * dom_count) ** (-0.5)
    source_ids = src_part[:, 0] * entities + src_row
    live = (jnp.arange(block_rows)[None, :] < block_valid[0][:, None]).reshape(edge_count)
    owners = jnp.broadcast_to(block_owner, (block_count, block_rows)).reshape(edge_count)
    target_ids = jnp.where(live, owners * entities + edge_dst, -1)
    relation_hot = onehot(edge_rel, 0, relations)
    table = lax.all_gather(feats, "dom", axis=1, tiled=True)
    source_quarter = pick(table, source_ids, chunk)
    gathered = lax.all_gather(
        jnp.concatenate([source_quarter, feats], axis=1), "feat", axis=0, tiled=True
    )
    sources = gathered[:, :edge_count]
    own_full = gathered[:, edge_count:]
    bases_flat = bases.reshape(basis_count * quarter, width)
    first = coef.astype(BF)
    second = (coef - first.astype(F32)).astype(BF)
    third = (coef - first.astype(F32) - second.astype(F32)).astype(BF)
    weights = (
        dot(first, relation_hot, 0, 0)
        + dot(second, relation_hot, 0, 0)
        + dot(third, relation_hot, 0, 0)
    )
    products = dot(bases_flat, sources, 1, 0).reshape(basis_count, quarter, edge_count)
    messages = jnp.sum(weights[:, None, :] * products, axis=0).astype(BF)
    extra = 16
    tail = jnp.zeros((extra, edge_count), BF).at[0].set(1.0)
    partial = spread(jnp.concatenate([messages, tail], axis=0), target_ids, total_entities, chunk)
    counted = partial[quarter : quarter + 1]
    high = jnp.floor(counted / 128.0)
    counts = jnp.concatenate(
        [high, counted - 128.0 * high, jnp.zeros((extra - 2, total_entities), F32)], axis=0
    )
    arrived = scatter_sum(
        jnp.concatenate([partial[:quarter], counts], axis=0).astype(BF), "dom", dom_count
    )
    aggregate = arrived[:quarter]
    degree = arrived[quarter : quarter + 1] * 128.0 + arrived[quarter + 1 : quarter + 2]
    inverse_degree = 1.0 / jnp.maximum(degree, 1.0)
    preact = dot(self_weight, own_full, 0, 0) + inverse_degree * aggregate
    output = jax.nn.silu(preact).astype(BF)
    sigmoid_pre = jax.nn.sigmoid(preact)
    grad_pre = (cotangent.astype(F32) * sigmoid_pre * (1.0 + preact * (1.0 - sigmoid_pre))).astype(
        BF
    )
    grad_node = (grad_pre.astype(F32) * inverse_degree).astype(BF)
    grad_table = lax.all_gather(grad_node, "dom", axis=1, tiled=True)
    grad_message = pick(grad_table, target_ids, chunk)
    grad_float = grad_message.astype(F32)
    scaled = jnp.sum(products * grad_float[None], axis=1)
    combined = (weights[:, None, :] * grad_float[None]).astype(BF)
    combined = combined.reshape(basis_count * quarter, edge_count)
    grad_bases = dot(combined, sources, 1, 1)
    edge_partial = dot(bases_flat, combined, 0, 0)
    self_partial = dot(self_weight, grad_pre, 1, 0)
    self_term = dot(grad_pre, own_full, 1, 1)
    both = jnp.concatenate([edge_partial, self_partial], axis=1).astype(BF)
    both = lax.all_to_all(both, "feat", split_axis=0, concat_axis=0, tiled=True)
    both = jnp.sum(both.reshape(feat_count, quarter, -1).astype(F32), axis=0)
    edge_grads = both[:, :edge_count].astype(BF)
    self_grads = both[:, edge_count:]
    node_grads = spread(edge_grads, source_ids, total_entities, chunk).astype(BF)
    grad_feats = (self_grads + scatter_sum(node_grads, "dom", dom_count)).astype(BF)
    stacked = jnp.concatenate([grad_bases, self_term], axis=0).astype(BF)
    pieces = lax.all_to_all(stacked, "dom", split_axis=0, concat_axis=0, tiled=True)
    piece = jnp.sum(pieces.reshape(dom_count, -1, width).astype(F32), axis=0) * scale
    whole = lax.all_gather(piece.astype(BF), "dom", axis=0, tiled=True).astype(F32)
    cut = basis_count * quarter
    scaled_high = scaled.astype(BF)
    scaled_low = (scaled - scaled_high.astype(F32)).astype(BF)
    grad_coef = dot(relation_hot, scaled_high, 1, 1) + dot(relation_hot, scaled_low, 1, 1)
    coef_total = lax.psum(grad_coef, ("dom", "feat"))
    return (
        output,
        grad_feats,
        whole[:cut].reshape(basis_count, quarter, width),
        whole[cut:].T,
        coef_total * scale,
    )


def solution(mesh):
    return jax.shard_map(
        body,
        mesh=mesh,
        in_specs=(
            P("feat", "dom"),
            P(None, "feat"),
            P(None, "feat", None),
            P(),
            P("dom", None),
            P("dom"),
            P("dom"),
            P("dom"),
            P("dom", None),
            P("dom", None),
            P("feat", "dom"),
        ),
        out_specs=(P("feat", "dom"), P("feat", "dom"), P(None, "feat", None), P(None, "feat"), P()),
        check_vma=False,
    )
```

profile of v0, /device:TPU:0, one launch (start us, length us, event | category | flops | bytes accessed | tf_op | source)
XLA Modules:
  0.0 253.4 jit_solution(16554198673092056434)
XLA Ops:
  0.6 0.0 copy-start
  0.6 0.0 copy-start.1
  0.7 1.2 fusion.18
  1.8 1.1 fusion.19
  2.9 0.7 broadcast_multiply_fusion.1
  3.6 33.2 %all_gather.12 = bf16[64,4096]{1,0:T(8,128)(2,1)S(1)} all-gather(bf16[64,512]{1,0:T(8,128)(2,1)} %param.13), channel_id=1, replica_groups=mesh['dom'=8,'feat'=4] {'dom'}, dimensions={1}, use_global_device_ids=true | all-gather | bytes 589824 | tf_op jit(solution)/shard_map/all_gather | solution.py:79
  36.9 0.7 add.36
  37.5 2.8 %fusion.13 = bf16[64,1024]{1,0:T(8,128)(2,1)S(1)} fusion(bf16[64,4096]{1,0:T(8,128)(2,1)S(1)} %all_gather.12, s32[1024]{0:T(1024)S(1)} %add.36), kind=kOutput, calls=%fused_computation.25 | convolution fusion | flops 541130752 | bytes 659456 | tf_op jit(solution)/shard_map/dot_general | solution.py:11
  40.3 0.0 copy-done.1
  40.3 8.6 %all_gather.13 = bf16[256,1536]{1,0:T(8,128)(2,1)S(1)} all-gather(bf16[64,1536]{1,0:T(8,128)(2,1)S(1)} %pad_maximum_fusion.2), channel_id=1, replica_groups=mesh['dom'=8,'feat'=4] {'feat'}, dimensions={0}, use_global_device_ids=true | all-gather | bytes 983040 | tf_op jit(solution)/shard_map/all_gather | solution.py:81
  49.0 0.0 copy-done
  49.0 4.5 %convolution_bitcast_fusion = f32[1920,1024]{0,1:T(8,128)} fusion(bf16[1920,256]{1,0:T(8,128)(2,1)S(1)} %bitcast.63, bf16[256,1536]{1,0:T(8,128)(2,1)S(1)} %all_gather.13), kind=kOutput, calls=%fused_computation.14 | convolution fusion | flops 1006632960 | bytes 9371648 | tf_op jit(solution)/shard_map/dot_general | solution.py:11
  53.4 9.1 %copy.19 = f32[1920,1024]{1,0:T(8,128)} copy(f32[1920,1024]{0,1:T(8,128)} %convolution_bitcast_fusion) | data formatting | bytes 15728640 | tf_op jit(solution)/shard_map/dot_general | solution.py:11
  62.5 0.0 copy-done.8
  62.5 0.0 copy-done.2
  62.5 0.0 copy-done.4
  62.5 0.0 copy-start.5
  62.6 0.0 copy-start.6
  62.6 0.0 copy-start.9
  62.6 0.3 fusion.15
  62.9 4.1 %multiply_reduce_fusion.1 = bf16[64,1024]{1,0:T(8,128)(2,1)S(1)} fusion(f32[30,64,1024]{2,1,0:T(8,128)} %bitcast.64, f32[30,1024]{1,0:T(8,128)S(1)} %fusion.15), kind=kLoop, calls=%fused_computation.12 | loop fusion | flops 3866624 | bytes 8118272 | tf_op jit(solution)/shard_map/reduce_sum | solution.py:96
  67.0 0.0 copy-done.5
  67.0 0.0 copy-done.6
  67.0 0.1 fusion.39
  67.1 0.0 copy-done.9
  67.1 3.4 %fusion.1 = f32[80,4096]{1,0:T(8,128)S(1)} fusion(s32[1024]{0:T(1024)S(1)} %fusion.39, bf16[16,1024]{1,0:T(8,128)(2,1)S(1)} %copy-done.9, bf16[64,1024]{1,0:T(8,128)(2,1)S(1)} %multiply_reduce_fusion.1), kind=kOutput, calls=%fused_computation.2 | convolution fusion | flops 675610624 | bytes 1478656 | tf_op jit(solution)/shard_map/dot_general | solution.py:11
  70.5 0.0 copy-start.3
  70.5 0.0 copy-start.7
  70.5 0.1 slice.101
  70.7 0.1 pad.9.clone
  70.7 0.2 maximum_maximum_fusion
  71.0 23.6 %all_to_all.35 = bf16[80,8,512]{2,0,1:T(8,128)(2,1)S(1)} all-to-all(bf16[80,8,512]{2,0,1:T(8,128)(2,1)S(1)} %maximum_maximum_fusion), channel_id=1, replica_groups=mesh['dom'=8,'feat'=4] {'dom'}, dimensions={1} | all-to-all | bytes 1310720 | tf_op jit(solution)/shard_map/all_to_all | solution.py:46
  94.6 0.1 convert_reduce_fusion.2
  94.7 0.0 copy-done.3
  94.7 0.0 copy-done.7
  94.7 0.9 multiply_convert_fusion.3
  95.6 31.8 %all_gather.14 = bf16[64,4096]{1,0:T(8,128)(2,1)S(1)} all-gather(bf16[64,512]{1,0:T(8,128)(2,1)S(1)} %get-tuple-element.17), channel_id=1, replica_groups=mesh['dom'=8,'feat'=4] {'dom'}, dimensions={1}, use_global_device_ids=true | all-gather | bytes 589824 | tf_op jit(solution)/shard_map/all_gather | solution.py:118
  127.4 3.2 %fusion.12 = f32[64,1024]{1,0:T(8,128)S(1)} fusion(bf16[64,4096]{1,0:T(8,128)(2,1)S(1)} %all_gather.14, s32[1024]{0:T(1024)S(1)} %fusion.39), kind=kOutput, calls=%fused_computation.24 | convolution fusion | flops 541196288 | bytes 790528 | tf_op jit(solution)/shard_map/dot_general | solution.py:11
  130.6 1.3 fusion.9
  131.9 0.3 convolution_convert_fusion.1
  132.1 0.1 pad_maximum_fusion.1
  132.2 14.0 %all_to_all.36 = bf16[4,64,1536]{2,1,0:T(8,128)(2,1)S(1)} all-to-all(bf16[4,64,1536]{2,1,0:T(8,128)(2,1)S(1)} %pad_maximum_fusion.1), channel_id=1, replica_groups=mesh['dom'=8,'feat'=4] {'feat'}, dimensions={0} | all-to-all | bytes 1572864 | tf_op jit(solution)/shard_map/all_to_all | solution.py:129
  146.2 0.1 convert_reduce_fusion.1
  146.4 3.4 %fusion.8 = bf16[64,4096]{1,0:T(8,128)(2,1)S(1)} fusion(s32[1024]{0:T(1024)S(1)} %add.36, f32[64,1536]{1,0:T(8,128)S(1)} %convert_reduce_fusion.1), kind=kOutput, calls=%fused_computation.13 | convolution fusion | flops 541327360 | bytes 659456 | tf_op jit(solution)/shard_map/dot_general | solution.py:11
  149.7 0.9 copy.28
  150.6 3.5 %all-to-all-start.2 = ((bf16[64,8,512]{2,0,1:T(8,128)(2,1)}), bf16[64,8,512]{2,0,1:T(8,128)(2,1)S(1)}, u32[]{:S(2)}, u32[]{:S(2)}) async-start(bf16[64,8,512]{2,0,1:T(8,128)(2,1)} %bitcast.61), calls=%async_computation.2 | async-start | bytes 1048576 | tf_op jit(solution)/shard_map/all_to_all | solution.py:46
  154.1 4.9 %multiply_reduce_fusion = (f32[30,1024]{1,0:T(8,128)S(1)}, bf16[30,64,1024]{2,1,0:T(8,128)(2,1)S(1)}) fusion(f32[30,64,1024]{2,1,0:T(8,128)} %bitcast.65, f32[64,1024]{1,0:T(8,128)S(1)} %fusion.12, f32[30,1024]{1,0:T(8,128)S(1)} %fusion.15), kind=kLoop, calls=%fused_computation.10 | loop fusion | flops 7833600 | bytes 12304384 | tf_op jit(solution)/shard_map/reduce_sum | solution.py:121
  159.0 0.2 convolution_convert_fusion.2
  159.2 1.3 convolution_convert_fusion
  160.5 1.0 pad_maximum_fusion
  161.5 6.9 %all-to-all-done.2 = bf16[64,8,512]{2,0,1:T(8,128)(2,1)S(1)} async-done(((bf16[64,8,512]{2,0,1:T(8,128)(2,1)}), bf16[64,8,512]{2,0,1:T(8,128)(2,1)S(1)}, u32[]{:S(2)}, u32[]{:S(2)}) %all-to-all-start.2) | async-done | bytes 524320 | tf_op jit(solution)/shard_map/all_to_all | solution.py:46
  168.4 3.6 %all-to-all-start.3 = ((bf16[8,248,256]{2,1,0:T(8,128)(2,1)}), bf16[8,248,256]{2,1,0:T(8,128)(2,1)S(1)}, u32[]{:S(2)}, u32[]{:S(2)}) async-start(bf16[8,248,256]{2,1,0:T(8,128)(2,1)} %bitcast.20), calls=%async_computation.3 | async-start | bytes 2031616 | tf_op jit(solution)/shard_map/all_to_all | solution.py:136
  172.0 0.3 fusion.17
  172.3 0.3 convolution_add_fusion
  172.6 44.3 %psum.7 = f32[237,30]{0,1:T(8,128)S(1)} all-reduce(f32[237,30]{0,1:T(8,128)S(1)} %convolution_add_fusion), channel_id=1, replica_groups=mesh['dom'=8,'feat'=4] {'dom','feat'}, use_global_device_ids=true, to_apply=%region_6.7 | all-reduce | flops 7110 | bytes 56880 | tf_op jit(solution)/shard_map/psum | solution.py:143
  216.8 0.6 broadcast_multiply_fusion
  217.5 0.1 convert_reduce_fusion.3
  217.5 0.7 fusion.32
  218.2 0.0 all-to-all-done.3
  218.2 0.1 convert_reduce_fusion
  218.4 32.9 %all_gather.15 = bf16[1984,256]{1,0:T(8,128)(2,1)S(1)} all-gather(bf16[248,256]{1,0:T(8,128)(2,1)S(1)} %multiply_convert_fusion.2), channel_id=1, replica_groups=mesh['dom'=8,'feat'=4] {'dom'}, dimensions={0}, use_global_device_ids=true | all-gather | bytes 1142784 | tf_op jit(solution)/shard_map/all_gather | solution.py:138
  251.2 0.2 convert_element_type.128
  251.4 1.4 slice.69
  252.8 0.6 slice_bitcast_fusion
  (10 shorter events, 0.1 us)
Async XLA Ops:
  0.6 48.3 %copy-start = (bf16[30,64,256]{2,1,0:T(8,128)(2,1)S(1)}, bf16[30,64,256]{2,1,0:T(8,128)(2,1)}, u32[]{:S(2)}) copy-start(bf16[30,64,256]{2,1,0:T(8,128)(2,1)} %param.15) | copy-start | bytes 2949124
  0.6 39.7 %copy-start.1 = (bf16[64,512]{1,0:T(8,128)(2,1)S(1)}, bf16[64,512]{1,0:T(8,128)(2,1)}, u32[]{:S(2)}) copy-start(bf16[64,512]{1,0:T(8,128)(2,1)} %param.13) | copy-start | bytes 196612
  53.4 9.1 %copy-start.8 = (s32[8,1]{0,1:T(1,128)S(1)}, s32[8,1]{0,1:T(1,128)}, u32[]{:S(2)}) copy-start(s32[8,1]{0,1:T(1,128)} %param.21) | copy-start | bytes 100
  53.4 9.1 %copy-start.2 = (f32[237,30]{0,1:T(8,128)S(1)}, f32[237,30]{0,1:T(8,128)}, u32[]{:S(2)}) copy-start(f32[237,30]{0,1:T(8,128)} %param.16) | copy-start | bytes 85324
  53.4 9.1 %copy-start.4 = (s32[1024]{0:T(1024)S(1)}, s32[1024]{0:T(1024)}, u32[]{:S(2)}) copy-start(s32[1024]{0:T(1024)} %param.20) | copy-start | bytes 12292
  62.5 4.5 %copy-start.5 = (s32[1024]{0:T(1024)S(1)}, s32[1024]{0:T(1024)}, u32[]{:S(2)}) copy-start(s32[1024]{0:T(1024)} %param.19) | copy-start | bytes 12292
  62.6 4.5 %copy-start.6 = (s32[1,8]{1,0:T(1,128)S(1)}, s32[1,8]{1,0:T(1,128)}, u32[]{:S(2)}) copy-start(s32[1,8]{1,0:T(1,128)} %param.22) | copy-start | bytes 100
  62.6 4.5 %copy-start.9 = (bf16[16,1024]{1,0:T(8,128)(2,1)S(1)}, bf16[16,1024]{1,0:T(8,128)(2,1)}, u32[]{:S(2)}) copy-start(bf16[16,1024]{1,0:T(8,128)(2,1)} %constant.47.clone.1) | copy-start | bytes 98308
  70.5 24.2 %copy-start.3 = (bf16[256,64]{0,1:T(8,128)(2,1)S(1)}, bf16[256,64]{0,1:T(8,128)(2,1)}, u32[]{:S(2)}) copy-start(bf16[256,64]{0,1:T(8,128)(2,1)} %param.14) | copy-start | bytes 98308
  70.5 24.2 %copy-start.7 = (bf16[64,512]{1,0:T(8,128)(2,1)S(1)}, bf16[64,512]{1,0:T(8,128)(2,1)}, u32[]{:S(2)}) copy-start(bf16[64,512]{1,0:T(8,128)(2,1)} %param.23) | copy-start | bytes 196612
  150.6 17.8 %all-to-all-start.2 = ((bf16[64,8,512]{2,0,1:T(8,128)(2,1)}), bf16[64,8,512]{2,0,1:T(8,128)(2,1)S(1)}, u32[]{:S(2)}, u32[]{:S(2)}) async-start(bf16[64,8,512]{2,0,1:T(8,128)(2,1)} %bitcast.61), calls=%async_computation.2 | async-start | bytes 1048576 | tf_op jit(solution)/shard_map/all_to_all | solution.py:46
  168.4 49.8 %all-to-all-start.3 = ((bf16[8,248,256]{2,1,0:T(8,128)(2,1)}), bf16[8,248,256]{2,1,0:T(8,128)(2,1)S(1)}, u32[]{:S(2)}, u32[]{:S(2)}) async-start(bf16[8,248,256]{2,1,0:T(8,128)(2,1)} %bitcast.20), calls=%async_computation.3 | async-start | bytes 2031616 | tf_op jit(solution)/shard_map/all_to_all | solution.py:136
where the time goes:
time: 254 us; the launch traced here: 253 us
  blocking collectives  188 us (74%)
  matrix products  24.1 us (9%)
  other arithmetic  13.7 us (5%)
  local copies, waits for them, and re-layouts  12.2 us (5%)
  starting transfers between devices  7.11 us (3%)
  waiting for transfers between devices  6.93 us (3%)
    psum x1, blocking collectives, body(): coef_total = lax.psum(grad_coef, ('dom', 'feat'))  44.3 us
    all_gather x1, blocking collectives, body(): table = lax.all_gather(feats, 'dom', axis=1, tiled=True)  33.2 us
    all_gather x1, blocking collectives, body(): lax.all_gather(piece.astype(BF), 'dom', axis=0, tiled=True).astype(F32)  32.9 us
    all_gather x1, blocking collectives, body(): grad_table = lax.all_gather(grad_node, 'dom', axis=1, tiled=True)  31.8 us
    dot_general x15, matrix products, dot(): lax.dot_general(left, right, (((left_axis,), (right_axis,)), ((), ())), p...  24.1 us
    all_to_all x1, blocking collectives, scatter_sum(): lax.all_to_all(values, axis, split_axis=1, concat_axis=0, tiled=True)  23.6 us
    all_to_all x1, blocking collectives, body(): both = lax.all_to_all(both, 'feat', split_axis=0, concat_axis=0, tiled=True)  14 us
    dot_general x1, local copies, waits for them, and re-layouts, dot(): lax.dot_general(left, right, (((left_axis,), (right_axis,)), ((), ())), p...  9.08 us
  transfers between devices with their start and end apart: 2, of which 1 were waited for; matrix products, arithmetic and copies ran while one was open for 4% of the time, Pallas kernels for 0%

commit v1 on v0

--- a/solution.py
+++ b/solution.py
@@ -140,7 +140,7 @@
     scaled_high = scaled.astype(BF)
     scaled_low = (scaled - scaled_high.astype(F32)).astype(BF)
     grad_coef = dot(relation_hot, scaled_high, 1, 1) + dot(relation_hot, scaled_low, 1, 1)
-    coef_total = lax.psum(grad_coef, ("dom", "feat"))
+    coef_total = jnp.sum(lax.all_gather(grad_coef, ("dom", "feat")), axis=0)
     return (
         output,
         grad_feats,

time: 254 us -> 266 us (1.047)
  blocking collectives: 188 us -> 199 us
    all_gather x0 -> x1, blocking collectives: none -> 54.4 us  [body(): coef_total = jnp.sum(lax.all_gather(grad_coef, ('dom', 'feat')), axis=0)]
    psum x1 -> x0, blocking collectives: 44.3 us -> none  [body(): coef_total = lax.psum(grad_coef, ('dom', 'feat'))]
where the time goes in v1:
time: 266 us
  blocking collectives  199 us (75%)
  matrix products  24.1 us (9%)
  other arithmetic  14.8 us (6%)
  local copies, waits for them, and re-layouts  12.3 us (5%)
  starting transfers between devices  7.76 us (3%)
  waiting for transfers between devices  7 us (3%)
    all_gather x1, blocking collectives, body(): coef_total = jnp.sum(lax.all_gather(grad_coef, ('dom', 'feat')), axis=0)  54.4 us
    all_gather x1, blocking collectives, body(): table = lax.all_gather(feats, 'dom', axis=1, tiled=True)  33.2 us
    all_gather x1, blocking collectives, body(): lax.all_gather(piece.astype(BF), 'dom', axis=0, tiled=True).astype(F32)  32.9 us
    all_gather x1, blocking collectives, body(): grad_table = lax.all_gather(grad_node, 'dom', axis=1, tiled=True)  31.8 us
    dot_general x15, matrix products, dot(): lax.dot_general(left, right, (((left_axis,), (right_axis,)), ((), ())), p...  24.1 us
    all_to_all x1, blocking collectives, scatter_sum(): lax.all_to_all(values, axis, split_axis=1, concat_axis=0, tiled=True)  23.6 us
    all_to_all x1, blocking collectives, body(): both = lax.all_to_all(both, 'feat', split_axis=0, concat_axis=0, tiled=True)  14 us
    dot_general x1, local copies, waits for them, and re-layouts, dot(): lax.dot_general(left, right, (((left_axis,), (right_axis,)), ((), ())), p...  9.08 us
  transfers between devices with their start and end apart: 2, of which 1 were waited for; matrix products, arithmetic and copies ran while one was open for 4% of the time, Pallas kernels for 0%

profile of v1, /device:TPU:0, one launch (start us, length us, event | category | flops | bytes accessed | tf_op | source)
XLA Modules:
  0.0 265.5 jit_solution(16788702208414730274)
XLA Ops:
  0.6 0.0 copy-start
  0.6 0.0 copy-start.1
  0.7 1.2 fusion.19
  1.8 1.1 fusion.20
  2.9 0.7 broadcast_multiply_fusion.1
  3.6 33.2 %all_gather.18 = bf16[64,4096]{1,0:T(8,128)(2,1)S(1)} all-gather(bf16[64,512]{1,0:T(8,128)(2,1)} %param.13), channel_id=1, replica_groups=mesh['dom'=8,'feat'=4] {'dom'}, dimensions={1}, use_global_device_ids=true | all-gather | bytes 589824 | tf_op jit(solution)/shard_map/all_gather | solution.py:79
  36.9 0.7 add.34
  37.5 2.8 %fusion.13 = bf16[64,1024]{1,0:T(8,128)(2,1)S(1)} fusion(bf16[64,4096]{1,0:T(8,128)(2,1)S(1)} %all_gather.18, s32[1024]{0:T(1024)S(1)} %add.34), kind=kOutput, calls=%fused_computation.25 | convolution fusion | flops 541130752 | bytes 659456 | tf_op jit(solution)/shard_map/dot_general | solution.py:11
  40.3 0.0 copy-done.1
  40.3 8.6 %all_gather.19 = bf16[256,1536]{1,0:T(8,128)(2,1)S(1)} all-gather(bf16[64,1536]{1,0:T(8,128)(2,1)S(1)} %pad_maximum_fusion.2), channel_id=1, replica_groups=mesh['dom'=8,'feat'=4] {'feat'}, dimensions={0}, use_global_device_ids=true | all-gather | bytes 983040 | tf_op jit(solution)/shard_map/all_gather | solution.py:81
  49.0 0.0 copy-done
  49.0 4.5 %convolution_bitcast_fusion = f32[1920,1024]{0,1:T(8,128)} fusion(bf16[1920,256]{1,0:T(8,128)(2,1)S(1)} %bitcast.65, bf16[256,1536]{1,0:T(8,128)(2,1)S(1)} %all_gather.19), kind=kOutput, calls=%fused_computation.14 | convolution fusion | flops 1006632960 | bytes 9371648 | tf_op jit(solution)/shard_map/dot_general | solution.py:11
  53.4 9.1 %copy.19 = f32[1920,1024]{1,0:T(8,128)} copy(f32[1920,1024]{0,1:T(8,128)} %convolution_bitcast_fusion) | data formatting | bytes 15728640 | tf_op jit(solution)/shard_map/dot_general | solution.py:11
  62.5 0.0 copy-done.8
  62.5 0.0 copy-done.2
  62.5 0.0 copy-done.4
  62.5 0.0 copy-start.5
  62.6 0.0 copy-start.6
  62.6 0.0 copy-start.9
  62.6 0.3 fusion.15
  62.9 4.1 %multiply_reduce_fusion.1 = bf16[64,1024]{1,0:T(8,128)(2,1)S(1)} fusion(f32[30,64,1024]{2,1,0:T(8,128)} %bitcast.66, f32[30,1024]{1,0:T(8,128)S(1)} %fusion.15), kind=kLoop, calls=%fused_computation.12 | loop fusion | flops 3866624 | bytes 8118272 | tf_op jit(solution)/shard_map/reduce_sum | solution.py:96
  67.0 0.0 copy-done.5
  67.0 0.0 copy-done.6
  67.0 0.1 fusion.40
  67.1 0.0 copy-done.9
  67.1 3.4 %fusion.1 = f32[80,4096]{1,0:T(8,128)S(1)} fusion(s32[1024]{0:T(1024)S(1)} %fusion.40, bf16[16,1024]{1,0:T(8,128)(2,1)S(1)} %copy-done.9, bf16[64,1024]{1,0:T(8,128)(2,1)S(1)} %multiply_reduce_fusion.1), kind=kOutput, calls=%fused_computation.2 | convolution fusion | flops 675610624 | bytes 1478656 | tf_op jit(solution)/shard_map/dot_general | solution.py:11
  70.5 0.0 copy-start.7
  70.5 0.1 slice.101
  70.7 0.1 pad.9.clone
  70.7 0.2 maximum_maximum_fusion
  71.0 23.6 %all_to_all.35 = bf16[80,8,512]{2,0,1:T(8,128)(2,1)S(1)} all-to-all(bf16[80,8,512]{2,0,1:T(8,128)(2,1)S(1)} %maximum_maximum_fusion), channel_id=1, replica_groups=mesh['dom'=8,'feat'=4] {'dom'}, dimensions={1} | all-to-all | bytes 1310720 | tf_op jit(solution)/shard_map/all_to_all | solution.py:46
  94.6 0.1 convert_reduce_fusion.2
  94.7 0.0 copy-done.3
  94.7 0.0 copy-done.7
  94.7 0.9 multiply_convert_fusion.3
  95.6 31.8 %all_gather.20 = bf16[64,4096]{1,0:T(8,128)(2,1)S(1)} all-gather(bf16[64,512]{1,0:T(8,128)(2,1)S(1)} %get-tuple-element.17), channel_id=1, replica_groups=mesh['dom'=8,'feat'=4] {'dom'}, dimensions={1}, use_global_device_ids=true | all-gather | bytes 589824 | tf_op jit(solution)/shard_map/all_gather | solution.py:118
  127.4 3.2 %fusion.12 = f32[64,1024]{1,0:T(8,128)S(1)} fusion(bf16[64,4096]{1,0:T(8,128)(2,1)S(1)} %all_gather.20, s32[1024]{0:T(1024)S(1)} %fusion.40), kind=kOutput, calls=%fused_computation.24 | convolution fusion | flops 541196288 | bytes 790528 | tf_op jit(solution)/shard_map/dot_general | solution.py:11
  130.6 1.3 fusion.9
  131.9 0.3 convolution_convert_fusion.1
  132.1 0.1 pad_maximum_fusion.1
  132.2 14.0 %all_to_all.36 = bf16[4,64,1536]{2,1,0:T(8,128)(2,1)S(1)} all-to-all(bf16[4,64,1536]{2,1,0:T(8,128)(2,1)S(1)} %pad_maximum_fusion.1), channel_id=1, replica_groups=mesh['dom'=8,'feat'=4] {'feat'}, dimensions={0} | all-to-all | bytes 1572864 | tf_op jit(solution)/shard_map/all_to_all | solution.py:129
  146.2 0.1 convert_reduce_fusion.1
  146.4 3.4 %fusion.8 = bf16[64,4096]{1,0:T(8,128)(2,1)S(1)} fusion(s32[1024]{0:T(1024)S(1)} %add.34, f32[64,1536]{1,0:T(8,128)S(1)} %convert_reduce_fusion.1), kind=kOutput, calls=%fused_computation.13 | convolution fusion | flops 541327360 | bytes 659456 | tf_op jit(solution)/shard_map/dot_general | solution.py:11
  149.7 0.9 copy.28
  150.6 4.1 %all-to-all-start.2 = ((bf16[64,8,512]{2,0,1:T(8,128)(2,1)}), bf16[64,8,512]{2,0,1:T(8,128)(2,1)}, u32[]{:S(2)}, u32[]{:S(2)}) async-start(bf16[64,8,512]{2,0,1:T(8,128)(2,1)} %bitcast.63), calls=%async_computation.2 | async-start | bytes 1048576 | tf_op jit(solution)/shard_map/all_to_all | solution.py:46
  154.8 4.9 %multiply_reduce_fusion = (f32[30,1024]{1,0:T(8,128)S(1)}, bf16[30,64,1024]{2,1,0:T(8,128)(2,1)S(1)}) fusion(f32[30,64,1024]{2,1,0:T(8,128)} %bitcast.67, f32[64,1024]{1,0:T(8,128)S(1)} %fusion.12, f32[30,1024]{1,0:T(8,128)S(1)} %fusion.15), kind=kLoop, calls=%fused_computation.10 | loop fusion | flops 7833600 | bytes 12304384 | tf_op jit(solution)/shard_map/reduce_sum | solution.py:121
  159.7 0.2 convolution_convert_fusion.2
  159.9 1.3 convolution_convert_fusion
  161.1 1.0 pad_maximum_fusion
  162.2 7.0 %all-to-all-done.2 = bf16[64,8,512]{2,0,1:T(8,128)(2,1)} async-done(((bf16[64,8,512]{2,0,1:T(8,128)(2,1)}), bf16[64,8,512]{2,0,1:T(8,128)(2,1)}, u32[]{:S(2)}, u32[]{:S(2)}) %all-to-all-start.2) | async-done | bytes 524320 | tf_op jit(solution)/shard_map/all_to_all | solution.py:46
  169.2 3.6 %all-to-all-start.3 = ((bf16[8,248,256]{2,1,0:T(8,128)(2,1)}), bf16[8,248,256]{2,1,0:T(8,128)(2,1)S(1)}, u32[]{:S(2)}, u32[]{:S(2)}) async-start(bf16[8,248,256]{2,1,0:T(8,128)(2,1)} %bitcast.20), calls=%async_computation.3 | async-start | bytes 2031616 | tf_op jit(solution)/shard_map/all_to_all | solution.py:136
  172.8 0.3 fusion.18
  173.1 0.3 fusion.17
  173.3 54.4 %all-gather.1 = f32[32,237,30]{1,2,0:T(8,128)S(1)} all-gather(f32[1,237,30]{1,2,0:T(8,128)S(1)} %fusion.17), channel_id=2, replica_groups=mesh['dom'=8,'feat'=4] {'dom','feat'}, dimensions={0}, use_global_device_ids=true | all-gather | bytes 938520 | tf_op jit(solution)/shard_map/all_gather | solution.py:143
  227.7 0.1 reduce_sum.69
  227.8 0.6 broadcast_multiply_fusion
  228.4 1.1 convert_reduce_fusion.3
  229.6 0.7 fusion.33
  230.2 0.0 all-to-all-done.3
  230.2 0.1 convert_reduce_fusion
  230.4 32.9 %all_gather.21 = bf16[1984,256]{1,0:T(8,128)(2,1)S(1)} all-gather(bf16[248,256]{1,0:T(8,128)(2,1)S(1)} %multiply_convert_fusion.2), channel_id=1, replica_groups=mesh['dom'=8,'feat'=4] {'dom'}, dimensions={0}, use_global_device_ids=true | all-gather | bytes 1142784 | tf_op jit(solution)/shard_map/all_gather | solution.py:138
  263.3 0.2 convert_element_type.128
  263.5 1.4 slice.69
  264.9 0.6 slice_bitcast_fusion
  (11 shorter events, 0.1 us)
Async XLA Ops:
  0.6 48.3 %copy-start = (bf16[30,64,256]{2,1,0:T(8,128)(2,1)S(1)}, bf16[30,64,256]{2,1,0:T(8,128)(2,1)}, u32[]{:S(2)}) copy-start(bf16[30,64,256]{2,1,0:T(8,128)(2,1)} %param.15) | copy-start | bytes 2949124
  0.6 39.7 %copy-start.1 = (bf16[64,512]{1,0:T(8,128)(2,1)S(1)}, bf16[64,512]{1,0:T(8,128)(2,1)}, u32[]{:S(2)}) copy-start(bf16[64,512]{1,0:T(8,128)(2,1)} %param.13) | copy-start | bytes 196612
  53.4 9.1 %copy-start.8 = (s32[8,1]{0,1:T(1,128)S(1)}, s32[8,1]{0,1:T(1,128)}, u32[]{:S(2)}) copy-start(s32[8,1]{0,1:T(1,128)} %param.21) | copy-start | bytes 100
  53.4 9.1 %copy-start.2 = (f32[237,30]{0,1:T(8,128)S(1)}, f32[237,30]{0,1:T(8,128)}, u32[]{:S(2)}) copy-start(f32[237,30]{0,1:T(8,128)} %param.16) | copy-start | bytes 85324
  53.4 9.1 %copy-start.4 = (s32[1024]{0:T(1024)S(1)}, s32[1024]{0:T(1024)}, u32[]{:S(2)}) copy-start(s32[1024]{0:T(1024)} %param.20) | copy-start | bytes 12292
  62.5 4.5 %copy-start.5 = (s32[1024]{0:T(1024)S(1)}, s32[1024]{0:T(1024)}, u32[]{:S(2)}) copy-start(s32[1024]{0:T(1024)} %param.19) | copy-start | bytes 12292
  62.6 4.5 %copy-start.6 = (s32[1,8]{1,0:T(1,128)S(1)}, s32[1,8]{1,0:T(1,128)}, u32[]{:S(2)}) copy-start(s32[1,8]{1,0:T(1,128)} %param.22) | copy-start | bytes 100
  62.6 4.5 %copy-start.9 = (bf16[16,1024]{1,0:T(8,128)(2,1)S(1)}, bf16[16,1024]{1,0:T(8,128)(2,1)}, u32[]{:S(2)}) copy-start(bf16[16,1024]{1,0:T(8,128)(2,1)} %constant.47.clone.1) | copy-start | bytes 98308
  70.5 24.2 %copy-start.3 = (bf16[256,64]{0,1:T(8,128)(2,1)S(1)}, bf16[256,64]{0,1:T(8,128)(2,1)}, u32[]{:S(2)}) copy-start(bf16[256,64]{0,1:T(8,128)(2,1)} %param.14) | copy-start | bytes 98308
  70.5 24.2 %copy-start.7 = (bf16[64,512]{1,0:T(8,128)(2,1)S(1)}, bf16[64,512]{1,0:T(8,128)(2,1)}, u32[]{:S(2)}) copy-start(bf16[64,512]{1,0:T(8,128)(2,1)} %param.23) | copy-start | bytes 196612
  150.6 18.5 %all-to-all-start.2 = ((bf16[64,8,512]{2,0,1:T(8,128)(2,1)}), bf16[64,8,512]{2,0,1:T(8,128)(2,1)}, u32[]{:S(2)}, u32[]{:S(2)}) async-start(bf16[64,8,512]{2,0,1:T(8,128)(2,1)} %bitcast.63), calls=%async_computation.2 | async-start | bytes 1048576 | tf_op jit(solution)/shard_map/all_to_all | solution.py:46
  169.2 61.1 %all-to-all-start.3 = ((bf16[8,248,256]{2,1,0:T(8,128)(2,1)}), bf16[8,248,256]{2,1,0:T(8,128)(2,1)S(1)}, u32[]{:S(2)}, u32[]{:S(2)}) async-start(bf16[8,248,256]{2,1,0:T(8,128)(2,1)} %bitcast.20), calls=%async_computation.3 | async-start | bytes 2031616 | tf_op jit(solution)/shard_map/all_to_all | solution.py:136
